TPU v7x, 32 devices: a whole 2x2x4 slice. The times are simulated.
32 devices in a mesh: ch: 4 (over z), sx: 4 (over x, core), sy: 2 (over y).
Axes of the slice: x: 2, y: 2, z: 4, core: 2. Of those that a mesh axis runs over, the one named last changes fastest.
Arguments:
- inputs: bfloat16 [768, 16, 4, 64], P('ch', 'sx', 'sy'), may hold values from -6 to 6
- pre_act: bfloat16 [768, 16, 4, 64], P('ch', 'sx', 'sy'), may hold values from -6 to 6
- out_grad: bfloat16 [768, 16, 4, 64], P('ch', 'sx', 'sy'), may hold values from -6 to 6
- weight_one: bfloat16 [27, 768, 768], P(None, 'ch'), may hold values from -0.0390625 to 0.0390625
- weight_two: bfloat16 [27, 768, 768], P(None, 'ch'), may hold values from -0.0390625 to 0.0390625
Outputs:
- input_grad: bfloat16 [768, 16, 4, 64], P('ch', 'sx', 'sy')
- filter_one_grad: float32 [27, 768, 768], P(None, 'ch')
- filter_two_grad: float32 [27, 768, 768], P(None, 'ch')
All inputs are finite; a program needn't handle non-finite values.
Results may differ from a plain program's by a relative error of at most 0.0049.
Values may be sent and summed in bfloat16 or wider, within the bound.
A program may use at most 192 MiB of HBM per device.

v0:
```python
import functools
import math

import jax
import jax.numpy as jnp
from jax import lax
from jax.experimental import pallas as pl
from jax.experimental.pallas import tpu as pltpu
from jax.sharding import PartitionSpec as P


def padded_2(cells, sides, width):
    for axis, dim in sides:
        count = lax.axis_size(axis)
        ends = count - 1
        head = lax.slice_in_dim(cells, 0, width, axis=dim)
        tail = lax.slice_in_dim(cells, cells.shape[dim] - width, cells.shape[dim], axis=dim)
        cells = jnp.concatenate(
            [
                lax.ppermute(tail, axis, [(i, (i + 1) % count) for i in range(ends)]),
                cells,
                lax.ppermute(head, axis, [((i + 1) % count, i) for i in range(ends)]),
            ],
            axis=dim,
        )
    return cells


def window(padded, offset, mirror):
    first = offset // 9
    second = offset // 3 % 3
    third = offset % 3
    if mirror:
        first, second, third = (2 - first, 2 - second, 2 - third)
    size_x = padded.shape[1] - 2
    size_y = padded.shape[2] - 2
    size_z = padded.shape[3] - 2
    part = padded[:, first : first + size_x, second : second + size_y, third : third + size_z]
    return part.reshape(padded.shape[0], size_x * size_y * size_z)


def pad_depth(array):
    return jnp.pad(array, ((0, 0), (0, 0), (0, 0), (1, 1)))


def contract_positions(left, right):
    return lax.dot_general(
        left, right, (((1,), (1,)), ((), ())), preferred_element_type=jnp.float32
    )


def contract_first(left, right):
    return lax.dot_general(
        left, right, (((0,), (0,)), ((), ())), preferred_element_type=jnp.float32
    )


def spread_flat(array):
    padded = jnp.pad(array, ((0, 0), (0, 0), (0, 1), (0, 1)))
    return padded.reshape(padded.shape[0], -1)


def whole_window(blocks, counts):
    count_x, count_y = counts
    channels, size_x, size_y, size_z = blocks.shape[1:]
    grid = blocks.reshape(count_x, count_y, channels, size_x, size_y, size_z)
    grid = grid.transpose(2, 0, 3, 1, 4, 5)
    return grid.reshape(channels, count_x * size_x, count_y * size_y, size_z)


def column_slices(full, counts):
    ranks = counts[0] * counts[1]
    cut = full.reshape(ranks, full.shape[0] // ranks, *full.shape[1:])
    return whole_window(lax.all_to_all(cut, ("sx", "sy"), 0, 0, tiled=True), counts)


def shifts(size_y, size_z):
    row = size_z + 1
    plane = (size_y + 1) * row
    return [
        (a - 1) * plane + (b - 1) * row + c - 1
        for a in range(3)
        for b in range(3)
        for c in range(3)
    ]


def filter_slice(rows, columns, shift_rows):
    steps = shifts(rows.shape[2], rows.shape[3])
    margin = max(steps)
    left = spread_flat(rows)
    size = left.shape[1]
    right = jnp.pad(spread_flat(columns), ((0, 0), (margin, margin)))
    out = []
    for step in steps:
        start = margin - step if shift_rows else margin + step
        part = lax.slice_in_dim(right, start, start + size, axis=1)
        out.append(contract_positions(left, part))
    return jnp.stack(out)


def join_columns(part, factor):
    sent = (part * factor).astype(jnp.bfloat16)
    parts = lax.all_gather(sent, ("sx", "sy"), axis=0)
    return jnp.concatenate([parts[i] for i in range(parts.shape[0])], axis=2).astype(jnp.float32)


def shards(inputs, pre_act, out_grad, weight_one, weight_two):
    shape = pre_act.shape
    positions = shape[1] * shape[2] * shape[3]
    counts = (lax.axis_size("sx"), lax.axis_size("sy"))
    factor = 1.0 / math.sqrt(positions * counts[0] * counts[1])
    full_grad = lax.all_gather(out_grad, "ch", axis=0, tiled=True)
    active = jnp.maximum(pre_act, jnp.zeros((), pre_act.dtype))
    active_all = whole_window(lax.all_gather(active, ("sx", "sy"), axis=0), counts)
    grad_columns = column_slices(full_grad, counts)
    grad_pad = pad_depth(padded_2(full_grad, (("sx", 1), ("sy", 2)), 1))
    filter_two = join_columns(filter_slice(active_all, grad_columns, True), factor)
    act_grad = jnp.zeros((shape[0], positions), jnp.float32)
    for offset in range(27):
        act_grad = act_grad + jnp.dot(
            weight_two[offset], window(grad_pad, offset, True), preferred_element_type=jnp.float32
        )
    delta = jnp.where(pre_act.reshape(shape[0], positions) > 0, act_grad, 0.0).astype(jnp.bfloat16)
    delta = delta.reshape(shape)
    full_in = lax.all_gather(inputs, "ch", axis=0, tiled=True)
    input_columns = column_slices(full_in, counts)
    delta_all = whole_window(lax.all_gather(delta, ("sx", "sy"), axis=0), counts)
    filter_one = join_columns(filter_slice(delta_all, input_columns, False), factor)
    delta_pad = pad_depth(padded_2(delta, (("sx", 1), ("sy", 2)), 1))
    partial_terms = jnp.zeros((weight_one.shape[2], positions), jnp.float32)
    for offset in range(27):
        partial_terms = partial_terms + contract_first(
            weight_one[offset], window(delta_pad, offset, True)
        )
    partial_terms = partial_terms.reshape(weight_one.shape[2], shape[1], shape[2], shape[3])
    input_grad = lax.psum_scatter(partial_terms, "ch", scatter_dimension=0, tiled=True).astype(
        jnp.bfloat16
    )
    return (input_grad, filter_one, filter_two)


F32 = jnp.float32
BF16 = jnp.bfloat16
MESH = pl.DeviceIdType.MESH
ANY = pl.BlockSpec(memory_space=pl.ANY)
IN_VMEM = pl.BlockSpec(memory_space=pltpu.VMEM)


def dot_lanes(left, right):
    return lax.dot_general(left, right, (((1,), (1,)), ((), ())), preferred_element_type=F32)


def lanes(shape):
    return lax.broadcasted_iota(jnp.int32, shape, len(shape) - 1)


def swap_halves(tile):
    return pltpu.roll(tile, tile.shape[-1] // 2, 1)


class Gather:
    def __init__(self, index, own, slot, half, send, recv, here):
        z, s, y = here
        flip = lax.rem(s + 2, 4)
        other = s + 1 - 2 * lax.rem(s, 2)
        other_flip = lax.rem(other + 2, 4)
        self.near = [(z, flip, y), (z, s, 1 - y), (z, other, y)]
        self.mine, self.from_x, self.from_y, self.from_d = (s, y), (flip, y), (s, 1 - y), (flip, 1 - y)
        self.pair = [(other, y), (other_flip, y), (other, 1 - y), (other_flip, 1 - y)]
        self.index, self.own, self.slot, self.half = index, own, slot, half
        self.send, self.recv = send, recv

    def copy(self, step, src, dst, to):
        return pltpu.make_async_remote_copy(
            src_ref=src,
            dst_ref=dst,
            send_sem=self.send.at[self.index, step],
            recv_sem=self.recv.at[self.index, step],
            device_id=self.near[to],
            device_id_type=MESH,
        )

    def sends(self):
        mine, slot, half = self.slot(self.mine), self.slot, self.half
        return [
            (0, self.own, mine, 0),
            (1, self.own, mine, 1),
            (2, self.own, mine, 2),
            (3, half(self.from_x, 0), half(self.from_x, 0), 1),
            (4, half(self.from_y, 1), half(self.from_y, 1), 0),
            (5, slot(self.from_x), slot(self.from_x), 2),
            (6, slot(self.from_y), slot(self.from_y), 2),
            (7, slot(self.from_d), slot(self.from_d), 2),
        ]

    def begin(self, steps):
        for entry in self.sends():
            if entry[0] in steps:
                self.copy(*entry).start()

    def arrive(self, step):
        where = {
            0: lambda: self.slot(self.from_x),
            1: lambda: self.slot(self.from_y),
            2: lambda: self.slot(self.pair[0]),
            3: lambda: self.half(self.from_d, 0),
            4: lambda: self.half(self.from_d, 1),
            5: lambda: self.slot(self.pair[1]),
            6: lambda: self.slot(self.pair[2]),
            7: lambda: self.slot(self.pair[3]),
        }[step]()
        self.copy(step, where, where, 0).wait_recv()

    def start(self):
        self.begin((0, 1, 2))

    def relay(self):
        self.arrive(0)
        self.begin((3, 5))
        self.arrive(1)
        self.begin((4, 6))

    def relay_far(self):
        self.arrive(3)
        self.arrive(4)
        self.begin((7,))

    def finish(self):
        for step in (2, 5, 6, 7):
            self.arrive(step)

    def drain(self):
        for entry in self.sends():
            self.copy(*entry).wait_send()


def fused_kernel(
    dims, factor,
    g_ref, in_ref, act_ref, w1_hbm, w2_hbm,
    ig_ref, pieces,
    acts, deltas, cols, full, edge, pack_s, pack_r, corner, tall, weight, shifted,
    facc, parts, cacc, dl, dpos, zacc, igt, term_s, term_r,
    ag_s, ag_r, c1_s, c1_r, c1_l, c2_s, c2_r, g_s, g_r, h_s, h_r, t_s, t_r, w_sem, o_sem,
):
    nch, nsx, nsy, rows, lx, ly, nz = dims
    lane = ly * nz
    nk = nsx * nsy
    piece = rows * nch // nk
    sub = piece // 2
    npos = lx * lane
    wide = nsy * lane
    z, s, y = lax.axis_index("ch"), lax.axis_index("sx"), lax.axis_index("sy")
    here = (z, s, y)
    mine = s * nsy + y
    parity = lax.rem(z, 2)
    core = lax.rem(s, 2)
    turn = z // 2

    barrier = pltpu.get_barrier_semaphore()
    for step in range(1, nk):
        k = lax.rem(mine + step, nk)
        pl.semaphore_signal(
            barrier, inc=1, device_id=(z, k // nsy, lax.rem(k, nsy)), device_id_type=MESH
        )
    for step in range(1, nch):
        pl.semaphore_signal(
            barrier, inc=1, device_id=(lax.rem(z + step, nch), s, y), device_id_type=MESH
        )
    pl.semaphore_wait(barrier, nk - 1 + nch - 1)

    load_two = pltpu.make_async_copy(w2_hbm, weight, w_sem.at[0])
    load_two.start()
    load_one = pltpu.make_async_copy(w1_hbm, weight, w_sem.at[1])

    def block_copy(op, ref, q):
        dst_s, dst_y = 2 * (q // 2) + parity, q % 2
        src = ref.at[:, pl.ds(q * sub, sub)]
        dst = cols.at[op, turn, mine]
        remote = pltpu.make_async_remote_copy(
            src_ref=src, dst_ref=dst, send_sem=c1_s.at[op, q], recv_sem=c1_r.at[op, mine],
            device_id=(z, dst_s, dst_y), device_id_type=MESH,
        )
        local = pltpu.make_async_copy(src, dst, c1_l.at[op])
        same = jnp.logical_and(dst_s == s, dst_y == y)
        return same, local, remote

    def blocks_start(op, ref):
        for q in range(nk // 2):
            same, local, remote = block_copy(op, ref, q)

            @pl.when(same)
            def _():
                local.start()

            @pl.when(jnp.logical_not(same))
            def _():
                remote.start()

    def blocks_wait(op, ref):
        @pl.when(parity == core)
        def _():
            for step in range(1, nk):
                k = lax.rem(mine + step, nk)
                dst = cols.at[op, turn, k]
                pltpu.make_async_remote_copy(
                    src_ref=dst, dst_ref=dst, send_sem=c1_s.at[op, 0], recv_sem=c1_r.at[op, k],
                    device_id=here, device_id_type=MESH,
                ).wait_recv()
        for q in range(nk // 2):
            same, local, remote = block_copy(op, ref, q)

            @pl.when(same)
            def _():
                local.wait()

    def blocks_drain(op, ref):
        for q in range(nk // 2):
            same, local, remote = block_copy(op, ref, q)

            @pl.when(jnp.logical_not(same))
            def _():
                remote.wait_send()

    def spread_copy(op, step):
        block = cols.at[op, turn]
        return pltpu.make_async_remote_copy(
            src_ref=block, dst_ref=block, send_sem=c2_s.at[op, step - 1], recv_sem=c2_r.at[op, turn],
            device_id=(lax.rem(z + step, nch), s, y), device_id_type=MESH,
        )

    def spread_start(op):
        @pl.when(parity == core)
        def _():
            for step in range(1, nch):
                spread_copy(op, step).start()

    def spread_wait(op):
        for t in range(2):
            @pl.when(core + 2 * t != z)
            def _():
                block = cols.at[op, t]
                pltpu.make_async_remote_copy(
                    src_ref=block, dst_ref=block, send_sem=c2_s.at[op, 0], recv_sem=c2_r.at[op, t],
                    device_id=here, device_id_type=MESH,
                ).wait_recv()

    def spread_drain(op):
        @pl.when(parity == core)
        def _():
            for step in range(1, nch):
                spread_copy(op, step).wait_send()

    def full_copy(step):
        return pltpu.make_async_remote_copy(
            src_ref=g_ref, dst_ref=full.at[z], send_sem=g_s.at[step - 1], recv_sem=g_r.at[z],
            device_id=(lax.rem(z + step, nch), s, y), device_id_type=MESH,
        )

    def whole(ref):
        slot = lambda k: ref.at[pl.ds(lx * k[0], lx), k[1]]
        half = lambda k, i: ref.at[pl.ds(lx * k[0] + i * (lx // 2), lx // 2), k[1]]
        return slot, half

    act_gather = Gather(0, act_ref, *whole(acts), ag_s, ag_r, here)
    delta_gather = Gather(1, dl, *whole(deltas), ag_s, ag_r, here)
    size = parts.shape[3]
    cut = size // 2 // 16 * 16

    def piece_gather(which, n):
        slot = lambda k: parts.at[which, n, k[0] * nsy + k[1]]
        half = lambda k, i: parts.at[
            which, n, k[0] * nsy + k[1], pl.ds(0, cut) if i == 0 else pl.ds(cut, size - cut)
        ]
        return Gather(2 + 9 * which + n, slot((s, y)), slot, half, ag_s, ag_r, here)

    blocks_start(0, g_ref)
    act_gather.start()
    blocks_start(1, in_ref)
    acts[pl.ds(lx * s, lx), y] = act_ref[...]
    full[z] = g_ref[...]
    blocks_wait(0, g_ref)
    spread_start(0)
    for step in range(1, nch):
        full_copy(step).start()
    act_gather.relay()
    blocks_wait(1, in_ref)
    spread_start(1)
    act_gather.relay_far()

    shifted[0] = jnp.zeros(shifted.shape[1:], BF16)
    shifted[shifted.shape[0] - 1] = jnp.zeros(shifted.shape[1:], BF16)

    def shift_columns(op):
        @pl.loop(0, nsx * lx)
        def _(p):
            owner, inner = p // lx, lax.rem(p, lx)
            tiles = [
                jnp.concatenate([cols[op, t, owner * nsy + j, inner] for t in range(2)], axis=0)
                for j in range(nsy)
            ]
            plane = jnp.concatenate(tiles, axis=1).astype(F32)
            where = lanes((piece, wide))
            row, depth = where // nz, lax.rem(where, nz)
            for b in range(3):
                for c in range(3):
                    move = (nz * (b - 1) + c - 1) % wide
                    value = pltpu.roll(plane, move, 1) if move else plane
                    keep = where >= 0
                    if b == 0:
                        keep = jnp.logical_and(keep, row < nsy * ly - 1)
                    if b == 2:
                        keep = jnp.logical_and(keep, row > 0)
                    if c == 0:
                        keep = jnp.logical_and(keep, depth < nz - 1)
                    if c == 2:
                        keep = jnp.logical_and(keep, depth > 0)
                    value = jnp.where(keep, value, 0.0).astype(BF16)
                    start = (3 * b + c) * piece
                    for j in range(nsy):
                        shifted[p + 1, j, pl.ds(start, piece)] = value[:, j * lane : (j + 1) * lane]

    def filter_pieces(which, left, first, last):
        @pl.loop(first, last)
        def _(a):
            facc[:, :rows] = jnp.zeros((facc.shape[0], rows), F32)

            @pl.loop(0, nsx)
            def _(o):
                cells = shifted[pl.ds(2 - a + lx * o, lx)]
                other = left[pl.ds(lx * o, lx)]
                cells = jnp.concatenate([cells[i, j] for i in range(lx) for j in range(nsy)], axis=1)
                other = jnp.concatenate([other[i, j] for i in range(lx) for j in range(nsy)], axis=1)
                facc[:, :rows] += dot_lanes(cells, other)

            group = 3 * piece
            for b in range(3):
                n = 3 * a + b
                main = facc[pl.ds(group * b, group), :lane] * factor
                parts[which, n, mine, pl.ds(0, group)] = main.astype(BF16)
                low = facc[pl.ds(group * b, group // 2), lane : 2 * lane] * factor
                high = facc[pl.ds(group * b + group // 2, group // 2), lane : 2 * lane] * factor
                both = jnp.where(lanes(low.shape) < rows - lane, low, swap_halves(high))
                parts[which, n, mine, pl.ds(group, group // 2)] = both.astype(BF16)
                piece_gather(which, n).start()

    def relay_pieces(which, first, last):
        @pl.loop(first, last)
        def _(n):
            piece_gather(which, n).relay()

    def write_piece(which, n):
        return pltpu.make_async_copy(parts.at[which, n], pieces.at[which, n], o_sem.at[which, n])

    def finish_pieces(which, first, last):
        @pl.loop(first, last)
        def _(n):
            piece_gather(which, n).relay_far()

        @pl.loop(first, last)
        def _(n):
            piece_gather(which, n).finish()
            write_piece(which, n).start()

    facc[...] = jnp.zeros(facc.shape, F32)
    act_gather.finish()
    spread_wait(0)
    shift_columns(0)
    filter_pieces(0, acts, 0, 3)

    for step in range(1, nch):
        k = lax.rem(z + step, nch)
        pltpu.make_async_remote_copy(
            src_ref=full.at[k], dst_ref=full.at[k], send_sem=g_s.at[0], recv_sem=g_r.at[k],
            device_id=here, device_id_type=MESH,
        ).wait_recv()

    low_half = lanes((rows, lane)) < nz
    for k in range(nch):
        for pair in range(lx // 2):
            first = full[k, 2 * pair].astype(F32)
            second = full[k, 2 * pair + 1].astype(F32)
            low = jnp.where(y == 0, swap_halves(first), first)
            high = jnp.where(y == 0, second, swap_halves(second))
            pack_s[k, pair] = jnp.where(low_half, low, high).astype(BF16)

    left_dev = (z, lax.rem(s + nsx - 1, nsx), y)
    right_dev = (z, lax.rem(s + 1, nsx), y)

    def halo(i, src, dst, dev):
        return pltpu.make_async_remote_copy(
            src_ref=src, dst_ref=dst, send_sem=h_s.at[i], recv_sem=h_r.at[i],
            device_id=dev, device_id_type=MESH,
        )

    to_y = halo(0, pack_s, pack_r, (z, s, 1 - y))
    to_left = halo(1, full.at[:, 0], edge.at[1], left_dev)
    to_right = halo(2, full.at[:, lx - 1], edge.at[0], right_dev)
    corner_left = halo(3, pack_r.at[:, 0], corner.at[1], left_dev)
    corner_right = halo(4, pack_r.at[:, lx // 2 - 1], corner.at[0], right_dev)
    has_left, has_right = s > 0, s < nsx - 1
    to_y.start()

    @pl.when(has_left)
    def _():
        to_left.start()

    @pl.when(has_right)
    def _():
        to_right.start()

    to_y.wait_recv()

    @pl.when(has_left)
    def _():
        corner_left.start()

    @pl.when(has_right)
    def _():
        corner_right.start()

    relay_pieces(0, 0, 9)

    @pl.when(has_right)
    def _():
        to_left.wait_recv()
        corner_left.wait_recv()

    @pl.when(has_left)
    def _():
        to_right.wait_recv()
        corner_right.wait_recv()

    for x in range(lx + 2):
        for k in range(nch):
            if x == 0:
                tile = jnp.where(has_left, edge[0, k].astype(F32), 0.0)
                beside = jnp.where(has_left, corner[0, k].astype(F32), 0.0)
                upper = True
            elif x == lx + 1:
                tile = jnp.where(has_right, edge[1, k].astype(F32), 0.0)
                beside = jnp.where(has_right, corner[1, k].astype(F32), 0.0)
                upper = False
            else:
                tile = full[k, x - 1].astype(F32)
                beside = pack_r[k, (x - 1) // 2].astype(F32)
                upper = (x - 1) % 2 == 1
            turned = swap_halves(beside)
            in_low, in_high = (turned, beside) if upper else (beside, turned)
            swapped = swap_halves(tile)
            above = jnp.where(low_half, swapped, jnp.where(y == 0, in_high, 0.0))
            below = jnp.where(low_half, jnp.where(y == 0, 0.0, in_low), swapped)
            tall[0, x, pl.ds(k * rows, rows)] = above.astype(BF16)
            tall[1, x, pl.ds(k * rows, rows)] = tile.astype(BF16)
            tall[2, x, pl.ds(k * rows, rows)] = below.astype(BF16)

    load_two.wait()
    cacc[...] = jnp.zeros(cacc.shape, F32)

    @pl.loop(0, 9)
    def _(ab):
        a, b = ab // 3, lax.rem(ab, 3)
        left = weight[pl.ds(3 * ab, 3)].reshape(3 * rows, nch * rows)
        right = tall[b, pl.ds(2 - a, lx)]
        right = jnp.concatenate([right[i] for i in range(lx)], axis=1)
        cacc[...] += jnp.dot(left, right, preferred_element_type=F32)

    load_one.start()
    depth = lax.rem(lanes((rows, lane)), nz)
    for x in range(lx):
        cut_x = slice(x * lane, (x + 1) * lane)
        total = cacc[rows : 2 * rows, cut_x]
        total += jnp.where(depth < nz - 1, pltpu.roll(cacc[:rows, cut_x], lane - 1, 1), 0.0)
        total += jnp.where(depth > 0, pltpu.roll(cacc[2 * rows :, cut_x], 1, 1), 0.0)
        total = jnp.where(act_ref[x].astype(F32) > 0.0, total, 0.0).astype(BF16)
        dl[x] = total
        deltas[lx * s + x, y] = total
    delta_gather.start()

    finish_pieces(0, 0, 9)
    spread_wait(1)
    shift_columns(1)
    delta_gather.relay()
    delta_gather.relay_far()
    delta_gather.finish()
    filter_pieces(1, deltas, 0, 3)

    for x in range(lx + 2):
        place = lx * s + x - 1
        inside = jnp.logical_and(place >= 0, place < nsx * lx)
        place = jnp.clip(place, 0, nsx * lx - 1)
        own = deltas[place, y].astype(F32).T
        beside = deltas[place, 1 - y].astype(F32).T
        own = jnp.where(inside, own, 0.0).astype(BF16)
        beside = jnp.where(inside, jnp.where(y == 0, beside[:nz], beside[lane - nz :]), 0.0)
        dpos[x, 0] = jnp.where(y == 0, 0.0, beside).astype(BF16)
        for j in range(ly):
            dpos[x, 1 + j] = own[j * nz : (j + 1) * nz]
        dpos[x, ly + 1] = jnp.where(y == 0, beside, 0.0).astype(BF16)

    zacc[...] = jnp.zeros(zacc.shape, F32)
    load_one.wait()

    @pl.loop(0, 9)
    def _(ab):
        a, b = ab // 3, lax.rem(ab, 3)
        left = dpos[pl.ds(2 - a, lx), pl.ds(2 - b, ly)].reshape(npos, rows)
        for c in range(3):
            zacc[c] += jnp.dot(left, weight[3 * ab + c], preferred_element_type=F32)

    for i in range(npos // nz):
        span = slice(i * nz, (i + 1) * nz)
        total = zacc[1, span]
        at = lax.broadcasted_iota(jnp.int32, total.shape, 0)
        total += jnp.where(at < nz - 1, pltpu.roll(zacc[0, span], nz - 1, 0), 0.0)
        total += jnp.where(at > 0, pltpu.roll(zacc[2, span], 1, 0), 0.0)
        igt[span] = total.astype(BF16)

    for k in range(nch):
        shape = (rows, nch * rows)
        pick = lanes(shape) == lax.broadcasted_iota(jnp.int32, shape, 0) + k * rows
        value = dot_lanes(pick.astype(BF16), igt[...]).astype(BF16)
        for x in range(lx):
            term_s[k, x] = value[:, x * lane : (x + 1) * lane]

    def term_copy(step):
        to = lax.rem(z + step, nch)
        return pltpu.make_async_remote_copy(
            src_ref=term_s.at[to], dst_ref=term_r.at[z], send_sem=t_s.at[step - 1],
            recv_sem=t_r.at[z], device_id=(to, s, y), device_id_type=MESH,
        )

    for step in range(1, nch):
        term_copy(step).start()
    relay_pieces(1, 0, 9)
    finish_pieces(1, 0, 9)

    total = term_s[z].astype(F32)
    for step in range(1, nch):
        k = lax.rem(z + step, nch)
        pltpu.make_async_remote_copy(
            src_ref=term_r.at[k], dst_ref=term_r.at[k], send_sem=t_s.at[0], recv_sem=t_r.at[k],
            device_id=here, device_id_type=MESH,
        ).wait_recv()
        total += term_r[k].astype(F32)
    ig_ref[...] = total.astype(BF16)

    for op, ref in ((0, g_ref), (1, in_ref)):
        blocks_drain(op, ref)
        spread_drain(op)
    for step in range(1, nch):
        full_copy(step).wait_send()
        term_copy(step).wait_send()
    to_y.wait_send()

    @pl.when(has_left)
    def _():
        to_left.wait_send()
        corner_left.wait_send()

    @pl.when(has_right)
    def _():
        to_right.wait_send()
        corner_right.wait_send()

    act_gather.drain()
    delta_gather.drain()
    for which in range(2):
        @pl.loop(0, 9)
        def _(n):
            piece_gather(which, n).drain()
            write_piece(which, n).wait()


def join_kernel(dims, two_ref, one_ref, out_two, out_one):
    nch, nsx, nsy, rows, lx, ly, nz = dims
    lane = ly * nz
    nk = nsx * nsy
    piece = rows * nch // nk
    sub = piece // 2
    group = 3 * piece
    rest = rows - lane
    shape = (lane, lane)
    same = (lanes(shape) == lax.broadcasted_iota(jnp.int32, shape, 0)).astype(BF16)
    shape = (rest, lane)
    down = lax.broadcasted_iota(jnp.int32, shape, 0)
    picks = [(lanes(shape) == down + i * rest).astype(BF16) for i in range(2)]
    for ref, out, mirror in ((two_ref, out_two, False), (one_ref, out_one, True)):
        for c in range(3):
            to = 2 - c if mirror else c
            main, tail = [], []
            for k in range(nch):
                for q in range(nk // 2):
                    slot = (2 * (q // 2) + k % 2) * nsy + q % 2
                    row = c * piece + (k // 2) * sub
                    main.append(ref[slot, row : row + sub])
                    row = group + (row if row < group // 2 else row - group // 2)
                    tail.append(ref[slot, row : row + sub])
            half = len(main) // 2
            for i in range(2):
                span = slice(i * half * sub, (i + 1) * half * sub)
                part = jnp.concatenate(main[i * half : (i + 1) * half], axis=0)
                out[to, :lane, span] = dot_lanes(same, part)
                part = jnp.concatenate(tail[i * half : (i + 1) * half], axis=0)
                upper = c * piece + i * sub >= group // 2
                out[to, lane:, span] = dot_lanes(picks[1 if upper else 0], part)


def tiles(array):
    rows, lx, ly, nz = array.shape
    return array.reshape(rows, lx, ly * nz).transpose(1, 0, 2)


def fused_shards(inputs, pre_act, out_grad, weight_one, weight_two):
    rows, lx, ly, nz = pre_act.shape
    nch, nsx, nsy = (lax.axis_size(axis) for axis in ("ch", "sx", "sy"))
    dims = (nch, nsx, nsy, rows, lx, ly, nz)
    lane = ly * nz
    nk = nsx * nsy
    channels = nch * rows
    piece = channels // nk
    npos = lx * lane
    factor = 1.0 / math.sqrt(npos * nk)
    size = 3 * piece * rows // lane
    planes = nsx * lx
    tile = (lx, rows, lane)
    vm = lambda *shape: pltpu.VMEM(shape, BF16)
    dma = lambda *shape: pltpu.SemaphoreType.DMA(shape)
    active = jnp.maximum(pre_act, jnp.zeros((), pre_act.dtype))
    grad, pieces = pl.pallas_call(
        functools.partial(fused_kernel, dims, factor),
        out_shape=(
            jax.ShapeDtypeStruct(tile, BF16),
            jax.ShapeDtypeStruct((2, 9, nk, size, lane), BF16),
        ),
        in_specs=[IN_VMEM] * 3 + [ANY] * 2,
        out_specs=(IN_VMEM, ANY),
        scratch_shapes=[
            vm(planes, nsy, rows, lane),
            vm(planes, nsy, rows, lane),
            vm(2, 2, nk, lx, piece // 2, lane),
            vm(nch, lx, rows, lane),
            vm(2, nch, rows, lane),
            vm(nch, lx // 2, rows, lane),
            vm(nch, lx // 2, rows, lane),
            vm(2, nch, rows, lane),
            vm(3, lx + 2, channels, lane),
            vm(27, rows, channels),
            vm(planes + 2, nsy, 9 * piece, lane),
            pltpu.VMEM((9 * piece, 2 * lane), F32),
            vm(2, 9, nk, size, lane),
            pltpu.VMEM((3 * rows, npos), F32),
            vm(lx, rows, lane),
            vm(lx + 2, ly + 2, nz, rows),
            pltpu.VMEM((3, npos, channels), F32),
            vm(npos, channels),
            vm(nch, lx, rows, lane),
            vm(nch, lx, rows, lane),
            dma(20, 8), dma(20, 8), dma(2, nk // 2), dma(2, nk), dma(2),
            dma(2, nch - 1), dma(2, 2), dma(nch - 1), dma(nch),
            dma(5), dma(5), dma(nch - 1), dma(nch), dma(2), dma(2, 9),
        ],
        compiler_params=pltpu.CompilerParams(
            collective_id=0, has_side_effects=True, vmem_limit_bytes=62 * 1024 * 1024
        ),
    )(tiles(out_grad), tiles(inputs), tiles(active), weight_one, weight_two)
    block = (None, None, nk, size, lane)
    two, one = pl.pallas_call(
        functools.partial(join_kernel, dims),
        grid=(9,),
        out_shape=(jax.ShapeDtypeStruct((27, rows, channels), F32),) * 2,
        in_specs=[
            pl.BlockSpec(block, lambda n: (0, n, 0, 0, 0)),
            pl.BlockSpec(block, lambda n: (1, n, 0, 0, 0)),
        ],
        out_specs=(
            pl.BlockSpec((3, rows, channels), lambda n: (n, 0, 0)),
            pl.BlockSpec((3, rows, channels), lambda n: (8 - n, 0, 0)),
        ),
        compiler_params=pltpu.CompilerParams(vmem_limit_bytes=40 * 1024 * 1024),
    )(pieces, pieces)
    grad = grad.transpose(1, 0, 2).reshape(rows, lx, ly, nz)
    return grad, one, two


def fits(mesh, rows, lx, ly, nz):
    nch, nsx, nsy = (mesh.shape[axis] for axis in ("ch", "sx", "sy"))
    return (
        (nch, nsx, nsy) == (4, 4, 2)
        and lx % 4 == 0
        and ly == 2
        and ly * nz == 128
        and rows % 64 == 0
        and 128 < rows < 256
    )


def solution(mesh):
    in_specs = (
        P("ch", "sx", "sy", None),
        P("ch", "sx", "sy", None),
        P("ch", "sx", "sy", None),
        P(None, "ch", None),
        P(None, "ch", None),
    )
    out_specs = (P("ch", "sx", "sy", None), P(None, "ch", None), P(None, "ch", None))

    def body(*args):
        return (fused_shards if fits(mesh, *args[1].shape) else shards)(*args)

    return jax.shard_map(body, mesh=mesh, in_specs=in_specs, out_specs=out_specs, check_vma=False)
```

profile of v0, /device:TPU:25, one launch (start us, length us, event | category | flops | bytes accessed | tf_op | source)
XLA Modules:
  0.0 159.2 jit_solution(1262105914171817341)
XLA Ops:
  0.6 1.0 broadcast_maximum_fusion
  1.6 0.8 copy.14
  2.4 1.8 %copy.12 = bf16[192,4,128]{2,0,1:T(8,128)(2,1)} copy(bf16[192,4,128]{0,2,1:T(8,128)(2,1)} %bitcast.12) | data formatting | bytes 393216 | tf_op jit(solution)/shard_map/reshape | solution.py:711
  4.2 1.8 %copy.13 = bf16[192,4,128]{2,0,1:T(8,128)(2,1)} copy(bf16[192,4,128]{0,2,1:T(8,128)(2,1)} %bitcast.13) | data formatting | bytes 393216 | tf_op jit(solution)/shard_map/reshape | solution.py:711
  5.9 132.7 %shard_map.76 = (bf16[4,192,128]{2,1,0:T(8,128)(2,1)}, bf16[2,9,8,432,128]{4,3,2,1,0:T(8,128)(2,1)}) custom-call(bf16[4,192,128]{2,1,0:T(8,128)(2,1)} %bitcast.10, bf16[4,192,128]{2,1,0:T(8,128)(2,1)} %bitcast.11, bf16[4,192,128]{2,1,0:T(8,128)(2,1)} %bitcast.9, bf16[27,192,768]{2,1,0:T(8,128)(2,1)} %w1_hbm.1, bf16[27,192,768]{2,1,0:T(8,128)(2,1)} %w2_hbm.1), custom_call_target="tpu_custom_call" | custom-call | tf_op jit(solution)/shard_map/pallas_call | solution.py:730
  138.7 0.0 copy-start
  138.7 19.6 %shard_map.77 = (f32[27,192,768]{2,1,0:T(8,128)}, f32[27,192,768]{2,1,0:T(8,128)}) custom-call(bf16[2,9,8,432,128]{4,3,2,1,0:T(8,128)(2,1)} %get-tuple-element.8.two_ref.one_ref, bf16[2,9,8,432,128]{4,3,2,1,0:T(8,128)(2,1)} %get-tuple-element.8.two_ref.one_ref), custom_call_target="tpu_custom_call" | custom-call | tf_op jit(solution)/shard_map/pallas_call | solution.py:768
  158.3 0.0 copy-done
  158.3 0.8 copy.15
Async XLA Ops:
  138.7 19.6 %copy-start = (bf16[4,192,128]{2,1,0:T(8,128)(2,1)S(1)}, bf16[4,192,128]{2,1,0:T(8,128)(2,1)}, u32[]{:S(2)}) copy-start(bf16[4,192,128]{2,1,0:T(8,128)(2,1)} %get-tuple-element.7) | copy-start | bytes 589828
where the time goes:
time: 160 us; the launch traced here: 159 us
  Pallas kernels  152 us (95%)
  local copies, waits for them, and re-layouts  5.2 us (3%)
    pallas_call x1, Pallas kernels, fused_shards(): pl.pallas_call(functools.partial(fused_kernel, dims, factor), out_shape=(...  133 us
    pallas_call x1, Pallas kernels, fused_shards(): pl.pallas_call(functools.partial(join_kernel, dims), grid=(9,), out_shape...  19.6 us
    reshape x3, local copies, waits for them, and re-layouts, tiles(): return array.reshape(rows, lx, ly * nz).transpose(1, 0, 2)  4.34 us

commit v1 on v0

--- a/solution.py
+++ b/solution.py
@@ -238,10 +238,10 @@
 def fused_kernel(
     dims, factor,
     g_ref, in_ref, act_ref, w1_hbm, w2_hbm,
-    ig_ref, pieces,
-    acts, deltas, cols, full, edge, pack_s, pack_r, corner, tall, weight, shifted,
-    facc, parts, cacc, dl, dpos, zacc, igt, term_s, term_r,
-    ag_s, ag_r, c1_s, c1_r, c1_l, c2_s, c2_r, g_s, g_r, h_s, h_r, t_s, t_r, w_sem, o_sem,
+    ig_ref, parts,
+    acts, deltas, cols, full, edge_s, edge_r, pack_s, pack_r, weight, shifted,
+    facc, cacc, near, dl, dpos, zacc, igt, term_s, term_r,
+    ag_s, ag_r, c1_s, c1_r, c1_l, c2_s, c2_r, g_s, g_r, h_s, h_r, t_s, t_r, w_sem,
 ):
     nch, nsx, nsy, rows, lx, ly, nz = dims
     lane = ly * nz
@@ -374,24 +374,27 @@
         ]
         return Gather(2 + 9 * which + n, slot((s, y)), slot, half, ag_s, ag_r, here)
 
-    blocks_start(0, g_ref)
-    act_gather.start()
-    blocks_start(1, in_ref)
-    acts[pl.ds(lx * s, lx), y] = act_ref[...]
-    full[z] = g_ref[...]
-    blocks_wait(0, g_ref)
-    spread_start(0)
-    for step in range(1, nch):
-        full_copy(step).start()
-    act_gather.relay()
-    blocks_wait(1, in_ref)
-    spread_start(1)
-    act_gather.relay_far()
-
-    shifted[0] = jnp.zeros(shifted.shape[1:], BF16)
-    shifted[shifted.shape[0] - 1] = jnp.zeros(shifted.shape[1:], BF16)
-
-    def shift_columns(op):
+    def clear():
+        for b in range(3):
+            for p in (0, nsx * lx + 1):
+                shifted[b, p] = jnp.zeros(shifted.shape[2:], BF16)
+        facc[...] = jnp.zeros(facc.shape, F32)
+        for b in range(3):
+            for x in range(lx + 2):
+                cacc[b, x] = jnp.zeros(cacc.shape[2:], F32)
+        zacc[...] = jnp.zeros(zacc.shape, F32)
+        acts[pl.ds(lx * s, lx), y] = act_ref[...]
+        full[z] = g_ref[...]
+
+    def start_full(beside):
+        for step in range(1, nch):
+            next_to = {1: z < nch - 1, nch - 1: z > 0}.get(step, z < 0)
+
+            @pl.when(next_to if beside else jnp.logical_not(next_to))
+            def _():
+                full_copy(step).start()
+
+    def shift_columns(op, b):
         @pl.loop(0, nsx * lx)
         def _(p):
             owner, inner = p // lx, lax.rem(p, lx)
@@ -402,87 +405,60 @@
             plane = jnp.concatenate(tiles, axis=1).astype(F32)
             where = lanes((piece, wide))
             row, depth = where // nz, lax.rem(where, nz)
-            for b in range(3):
-                for c in range(3):
-                    move = (nz * (b - 1) + c - 1) % wide
-                    value = pltpu.roll(plane, move, 1) if move else plane
-                    keep = where >= 0
-                    if b == 0:
-                        keep = jnp.logical_and(keep, row < nsy * ly - 1)
-                    if b == 2:
-                        keep = jnp.logical_and(keep, row > 0)
-                    if c == 0:
-                        keep = jnp.logical_and(keep, depth < nz - 1)
-                    if c == 2:
-                        keep = jnp.logical_and(keep, depth > 0)
-                    value = jnp.where(keep, value, 0.0).astype(BF16)
-                    start = (3 * b + c) * piece
-                    for j in range(nsy):
-                        shifted[p + 1, j, pl.ds(start, piece)] = value[:, j * lane : (j + 1) * lane]
-
-    def filter_pieces(which, left, first, last):
-        @pl.loop(first, last)
+            for c in range(3):
+                move = (nz * (b - 1) + c - 1) % wide
+                value = pltpu.roll(plane, move, 1) if move else plane
+                keep = where >= 0
+                if b == 0:
+                    keep = jnp.logical_and(keep, row < nsy * ly - 1)
+                if b == 2:
+                    keep = jnp.logical_and(keep, row > 0)
+                if c == 0:
+                    keep = jnp.logical_and(keep, depth < nz - 1)
+                if c == 2:
+                    keep = jnp.logical_and(keep, depth > 0)
+                value = jnp.where(keep, value, 0.0).astype(BF16)
+                for j in range(nsy):
+                    shifted[b, p + 1, j, pl.ds(c * piece, piece)] = value[:, j * lane : (j + 1) * lane]
+
+    def filter_pieces(which, left, b):
+        @pl.loop(0, 3)
         def _(a):
             facc[:, :rows] = jnp.zeros((facc.shape[0], rows), F32)
 
             @pl.loop(0, nsx)
             def _(o):
-                cells = shifted[pl.ds(2 - a + lx * o, lx)]
+                cells = shifted[b, pl.ds(2 - a + lx * o, lx)]
                 other = left[pl.ds(lx * o, lx)]
                 cells = jnp.concatenate([cells[i, j] for i in range(lx) for j in range(nsy)], axis=1)
                 other = jnp.concatenate([other[i, j] for i in range(lx) for j in range(nsy)], axis=1)
                 facc[:, :rows] += dot_lanes(cells, other)
 
             group = 3 * piece
-            for b in range(3):
-                n = 3 * a + b
-                main = facc[pl.ds(group * b, group), :lane] * factor
-                parts[which, n, mine, pl.ds(0, group)] = main.astype(BF16)
-                low = facc[pl.ds(group * b, group // 2), lane : 2 * lane] * factor
-                high = facc[pl.ds(group * b + group // 2, group // 2), lane : 2 * lane] * factor
-                both = jnp.where(lanes(low.shape) < rows - lane, low, swap_halves(high))
-                parts[which, n, mine, pl.ds(group, group // 2)] = both.astype(BF16)
-                piece_gather(which, n).start()
-
-    def relay_pieces(which, first, last):
-        @pl.loop(first, last)
-        def _(n):
-            piece_gather(which, n).relay()
-
-    def write_piece(which, n):
-        return pltpu.make_async_copy(parts.at[which, n], pieces.at[which, n], o_sem.at[which, n])
+            n = 3 * a + b
+            parts[which, n, mine, pl.ds(0, group)] = (facc[:, :lane] * factor).astype(BF16)
+            low = facc[: group // 2, lane : 2 * lane] * factor
+            high = facc[group // 2 :, lane : 2 * lane] * factor
+            both = jnp.where(lanes(low.shape) < rows - lane, low, swap_halves(high))
+            parts[which, n, mine, pl.ds(group, group // 2)] = both.astype(BF16)
+            piece_gather(which, n).start()
+
+    def relay_pieces(which, b):
+        @pl.loop(0, 3)
+        def _(a):
+            piece_gather(which, 3 * a + b).relay()
+
+    def far_pieces(which, b):
+        @pl.loop(0, 3)
+        def _(a):
+            piece_gather(which, 3 * a + b).relay_far()
 
     def finish_pieces(which, first, last):
         @pl.loop(first, last)
         def _(n):
-            piece_gather(which, n).relay_far()
-
-        @pl.loop(first, last)
-        def _(n):
             piece_gather(which, n).finish()
-            write_piece(which, n).start()
-
-    facc[...] = jnp.zeros(facc.shape, F32)
-    act_gather.finish()
-    spread_wait(0)
-    shift_columns(0)
-    filter_pieces(0, acts, 0, 3)
-
-    for step in range(1, nch):
-        k = lax.rem(z + step, nch)
-        pltpu.make_async_remote_copy(
-            src_ref=full.at[k], dst_ref=full.at[k], send_sem=g_s.at[0], recv_sem=g_r.at[k],
-            device_id=here, device_id_type=MESH,
-        ).wait_recv()
 
     low_half = lanes((rows, lane)) < nz
-    for k in range(nch):
-        for pair in range(lx // 2):
-            first = full[k, 2 * pair].astype(F32)
-            second = full[k, 2 * pair + 1].astype(F32)
-            low = jnp.where(y == 0, swap_halves(first), first)
-            high = jnp.where(y == 0, second, swap_halves(second))
-            pack_s[k, pair] = jnp.where(low_half, low, high).astype(BF16)
 
     left_dev = (z, lax.rem(s + nsx - 1, nsx), y)
     right_dev = (z, lax.rem(s + 1, nsx), y)
@@ -494,134 +470,9 @@
         )
 
     to_y = halo(0, pack_s, pack_r, (z, s, 1 - y))
-    to_left = halo(1, full.at[:, 0], edge.at[1], left_dev)
-    to_right = halo(2, full.at[:, lx - 1], edge.at[0], right_dev)
-    corner_left = halo(3, pack_r.at[:, 0], corner.at[1], left_dev)
-    corner_right = halo(4, pack_r.at[:, lx // 2 - 1], corner.at[0], right_dev)
+    to_left = halo(1, edge_s.at[0], edge_r.at[1], left_dev)
+    to_right = halo(2, edge_s.at[1], edge_r.at[0], right_dev)
     has_left, has_right = s > 0, s < nsx - 1
-    to_y.start()
-
-    @pl.when(has_left)
-    def _():
-        to_left.start()
-
-    @pl.when(has_right)
-    def _():
-        to_right.start()
-
-    to_y.wait_recv()
-
-    @pl.when(has_left)
-    def _():
-        corner_left.start()
-
-    @pl.when(has_right)
-    def _():
-        corner_right.start()
-
-    relay_pieces(0, 0, 9)
-
-    @pl.when(has_right)
-    def _():
-        to_left.wait_recv()
-        corner_left.wait_recv()
-
-    @pl.when(has_left)
-    def _():
-        to_right.wait_recv()
-        corner_right.wait_recv()
-
-    for x in range(lx + 2):
-        for k in range(nch):
-            if x == 0:
-                tile = jnp.where(has_left, edge[0, k].astype(F32), 0.0)
-                beside = jnp.where(has_left, corner[0, k].astype(F32), 0.0)
-                upper = True
-            elif x == lx + 1:
-                tile = jnp.where(has_right, edge[1, k].astype(F32), 0.0)
-                beside = jnp.where(has_right, corner[1, k].astype(F32), 0.0)
-                upper = False
-            else:
-                tile = full[k, x - 1].astype(F32)
-                beside = pack_r[k, (x - 1) // 2].astype(F32)
-                upper = (x - 1) % 2 == 1
-            turned = swap_halves(beside)
-            in_low, in_high = (turned, beside) if upper else (beside, turned)
-            swapped = swap_halves(tile)
-            above = jnp.where(low_half, swapped, jnp.where(y == 0, in_high, 0.0))
-            below = jnp.where(low_half, jnp.where(y == 0, 0.0, in_low), swapped)
-            tall[0, x, pl.ds(k * rows, rows)] = above.astype(BF16)
-            tall[1, x, pl.ds(k * rows, rows)] = tile.astype(BF16)
-            tall[2, x, pl.ds(k * rows, rows)] = below.astype(BF16)
-
-    load_two.wait()
-    cacc[...] = jnp.zeros(cacc.shape, F32)
-
-    @pl.loop(0, 9)
-    def _(ab):
-        a, b = ab // 3, lax.rem(ab, 3)
-        left = weight[pl.ds(3 * ab, 3)].reshape(3 * rows, nch * rows)
-        right = tall[b, pl.ds(2 - a, lx)]
-        right = jnp.concatenate([right[i] for i in range(lx)], axis=1)
-        cacc[...] += jnp.dot(left, right, preferred_element_type=F32)
-
-    load_one.start()
-    depth = lax.rem(lanes((rows, lane)), nz)
-    for x in range(lx):
-        cut_x = slice(x * lane, (x + 1) * lane)
-        total = cacc[rows : 2 * rows, cut_x]
-        total += jnp.where(depth < nz - 1, pltpu.roll(cacc[:rows, cut_x], lane - 1, 1), 0.0)
-        total += jnp.where(depth > 0, pltpu.roll(cacc[2 * rows :, cut_x], 1, 1), 0.0)
-        total = jnp.where(act_ref[x].astype(F32) > 0.0, total, 0.0).astype(BF16)
-        dl[x] = total
-        deltas[lx * s + x, y] = total
-    delta_gather.start()
-
-    finish_pieces(0, 0, 9)
-    spread_wait(1)
-    shift_columns(1)
-    delta_gather.relay()
-    delta_gather.relay_far()
-    delta_gather.finish()
-    filter_pieces(1, deltas, 0, 3)
-
-    for x in range(lx + 2):
-        place = lx * s + x - 1
-        inside = jnp.logical_and(place >= 0, place < nsx * lx)
-        place = jnp.clip(place, 0, nsx * lx - 1)
-        own = deltas[place, y].astype(F32).T
-        beside = deltas[place, 1 - y].astype(F32).T
-        own = jnp.where(inside, own, 0.0).astype(BF16)
-        beside = jnp.where(inside, jnp.where(y == 0, beside[:nz], beside[lane - nz :]), 0.0)
-        dpos[x, 0] = jnp.where(y == 0, 0.0, beside).astype(BF16)
-        for j in range(ly):
-            dpos[x, 1 + j] = own[j * nz : (j + 1) * nz]
-        dpos[x, ly + 1] = jnp.where(y == 0, beside, 0.0).astype(BF16)
-
-    zacc[...] = jnp.zeros(zacc.shape, F32)
-    load_one.wait()
-
-    @pl.loop(0, 9)
-    def _(ab):
-        a, b = ab // 3, lax.rem(ab, 3)
-        left = dpos[pl.ds(2 - a, lx), pl.ds(2 - b, ly)].reshape(npos, rows)
-        for c in range(3):
-            zacc[c] += jnp.dot(left, weight[3 * ab + c], preferred_element_type=F32)
-
-    for i in range(npos // nz):
-        span = slice(i * nz, (i + 1) * nz)
-        total = zacc[1, span]
-        at = lax.broadcasted_iota(jnp.int32, total.shape, 0)
-        total += jnp.where(at < nz - 1, pltpu.roll(zacc[0, span], nz - 1, 0), 0.0)
-        total += jnp.where(at > 0, pltpu.roll(zacc[2, span], 1, 0), 0.0)
-        igt[span] = total.astype(BF16)
-
-    for k in range(nch):
-        shape = (rows, nch * rows)
-        pick = lanes(shape) == lax.broadcasted_iota(jnp.int32, shape, 0) + k * rows
-        value = dot_lanes(pick.astype(BF16), igt[...]).astype(BF16)
-        for x in range(lx):
-            term_s[k, x] = value[:, x * lane : (x + 1) * lane]
 
     def term_copy(step):
         to = lax.rem(z + step, nch)
@@ -630,20 +481,195 @@
             recv_sem=t_r.at[z], device_id=(to, s, y), device_id_type=MESH,
         )
 
-    for step in range(1, nch):
-        term_copy(step).start()
-    relay_pieces(1, 0, 9)
+    def wait_full():
+        for step in range(1, nch):
+            k = lax.rem(z + step, nch)
+            pltpu.make_async_remote_copy(
+                src_ref=full.at[k], dst_ref=full.at[k], send_sem=g_s.at[0], recv_sem=g_r.at[k],
+                device_id=here, device_id_type=MESH,
+            ).wait_recv()
+
+    def act_grad():
+        load_two.wait()
+
+        @pl.loop(0, 9)
+        def _(ab):
+            a, b = ab // 3, lax.rem(ab, 3)
+            left = weight[pl.ds(3 * ab, 3)].reshape(3 * rows, nch * rows)
+            right = jnp.concatenate(
+                [jnp.concatenate([full[k, x] for x in range(lx)], axis=1) for k in range(nch)], axis=0
+            )
+            value = jnp.dot(left, right, preferred_element_type=F32)
+            for x in range(lx):
+                cacc[b, a + x] += value[:, x * lane : (x + 1) * lane]
+
+        load_one.start()
+
+    def fold_halo():
+        depth = lax.rem(lanes((rows, lane)), nz)
+        low = None
+        for x in range(lx + 2):
+            sums = []
+            for b in range(3):
+                total = cacc[b, x, pl.ds(rows, rows)]
+                back = pltpu.roll(cacc[b, x, pl.ds(0, rows)], lane - 1, 1)
+                ahead = pltpu.roll(cacc[b, x, pl.ds(2 * rows, rows)], 1, 1)
+                total += jnp.where(depth < nz - 1, back, 0.0)
+                total += jnp.where(depth > 0, ahead, 0.0)
+                sums.append(total)
+            up, down = swap_halves(sums[0]), swap_halves(sums[2])
+            near[x] = sums[1] + jnp.where(low_half, up, down)
+            if x % 2 == 0:
+                low = jnp.where(y == 0, down, sums[0])
+            else:
+                high = jnp.where(y == 0, sums[2], up)
+                pack_s[x // 2] = jnp.where(low_half, low, high).astype(BF16)
+        to_y.start()
+
+    def fold_edges():
+        to_y.wait_recv()
+        for x in range(lx + 2):
+            value = pack_r[x // 2].astype(F32)
+            turned = swap_halves(value)
+            to_high, to_low = (turned, value) if x % 2 == 0 else (value, turned)
+            high = jnp.where(low_half, 0.0, to_high)
+            low = jnp.where(low_half, to_low, 0.0)
+            near[x] += jnp.where(y == 0, high, low)
+        edge_s[0] = near[0].astype(BF16)
+        edge_s[1] = near[lx + 1].astype(BF16)
+
+        @pl.when(has_left)
+        def _():
+            to_left.start()
+
+        @pl.when(has_right)
+        def _():
+            to_right.start()
+
+    def make_delta():
+        @pl.when(has_right)
+        def _():
+            to_left.wait_recv()
+            near[lx] += edge_r[1].astype(F32)
+
+        @pl.when(has_left)
+        def _():
+            to_right.wait_recv()
+            near[1] += edge_r[0].astype(F32)
+
+        for x in range(lx):
+            total = jnp.where(act_ref[x].astype(F32) > 0.0, near[x + 1], 0.0).astype(BF16)
+            dl[x] = total
+            deltas[lx * s + x, y] = total
+        delta_gather.start()
+
+    def place_delta():
+        for x in range(lx + 2):
+            place = lx * s + x - 1
+            inside = jnp.logical_and(place >= 0, place < nsx * lx)
+            place = jnp.clip(place, 0, nsx * lx - 1)
+            own = deltas[place, y].astype(F32).T
+            beside = deltas[place, 1 - y].astype(F32).T
+            own = jnp.where(inside, own, 0.0).astype(BF16)
+            beside = jnp.where(inside, jnp.where(y == 0, beside[:nz], beside[lane - nz :]), 0.0)
+            dpos[x, 0] = jnp.where(y == 0, 0.0, beside).astype(BF16)
+            for j in range(ly):
+                dpos[x, 1 + j] = own[j * nz : (j + 1) * nz]
+            dpos[x, ly + 1] = jnp.where(y == 0, beside, 0.0).astype(BF16)
+
+    def input_terms():
+        load_one.wait()
+
+        @pl.loop(0, 9)
+        def _(ab):
+            a, b = ab // 3, lax.rem(ab, 3)
+            left = dpos[pl.ds(2 - a, lx), pl.ds(2 - b, ly)].reshape(npos, rows)
+            for c in range(3):
+                zacc[c] += jnp.dot(left, weight[3 * ab + c], preferred_element_type=F32)
+
+    def pack_terms():
+        for i in range(npos // nz):
+            span = slice(i * nz, (i + 1) * nz)
+            total = zacc[1, span]
+            at = lax.broadcasted_iota(jnp.int32, total.shape, 0)
+            total += jnp.where(at < nz - 1, pltpu.roll(zacc[0, span], nz - 1, 0), 0.0)
+            total += jnp.where(at > 0, pltpu.roll(zacc[2, span], 1, 0), 0.0)
+            igt[span] = total.astype(BF16)
+
+        for k in range(nch):
+            shape = (rows, nch * rows)
+            pick = lanes(shape) == lax.broadcasted_iota(jnp.int32, shape, 0) + k * rows
+            value = dot_lanes(pick.astype(BF16), igt[...]).astype(BF16)
+            for x in range(lx):
+                term_s[k, x] = value[:, x * lane : (x + 1) * lane]
+
+    def send_terms():
+        for step in range(1, nch):
+            term_copy(step).start()
+
+    def sum_terms():
+        total = term_s[z].astype(F32)
+        for step in range(1, nch):
+            k = lax.rem(z + step, nch)
+            pltpu.make_async_remote_copy(
+                src_ref=term_r.at[k], dst_ref=term_r.at[k], send_sem=t_s.at[0], recv_sem=t_r.at[k],
+                device_id=here, device_id_type=MESH,
+            ).wait_recv()
+            total += term_r[k].astype(F32)
+        ig_ref[...] = total.astype(BF16)
+
+    blocks_start(0, g_ref)
+    act_gather.start()
+    start_full(True)
+    blocks_start(1, in_ref)
+    blocks_wait(0, g_ref)
+    spread_start(0)
+    clear()
+    act_gather.relay()
+    act_gather.relay_far()
+    act_gather.finish()
+    spread_wait(0)
+    start_full(False)
+    shift_columns(0, 1)
+    filter_pieces(0, acts, 1)
+    shift_columns(0, 2)
+    filter_pieces(0, acts, 2)
+    relay_pieces(0, 1)
+    shift_columns(0, 0)
+    blocks_wait(1, in_ref)
+    wait_full()
+    spread_start(1)
+    act_grad()
+    fold_halo()
+    relay_pieces(0, 2)
+    fold_edges()
+    make_delta()
+    filter_pieces(0, acts, 0)
+    delta_gather.relay()
+    spread_wait(1)
+    shift_columns(1, 1)
+    delta_gather.relay_far()
+    relay_pieces(0, 0)
+    shift_columns(1, 2)
+    delta_gather.finish()
+    filter_pieces(1, deltas, 1)
+    filter_pieces(1, deltas, 2)
+    shift_columns(1, 0)
+    for b in (1, 2, 0):
+        far_pieces(0, b)
+    relay_pieces(1, 1)
+    place_delta()
+    input_terms()
+    pack_terms()
+    send_terms()
+    finish_pieces(0, 0, 9)
+    filter_pieces(1, deltas, 0)
+    relay_pieces(1, 2)
+    relay_pieces(1, 0)
+    for b in range(3):
+        far_pieces(1, (b + 1) % 3)
     finish_pieces(1, 0, 9)
-
-    total = term_s[z].astype(F32)
-    for step in range(1, nch):
-        k = lax.rem(z + step, nch)
-        pltpu.make_async_remote_copy(
-            src_ref=term_r.at[k], dst_ref=term_r.at[k], send_sem=t_s.at[0], recv_sem=t_r.at[k],
-            device_id=here, device_id_type=MESH,
-        ).wait_recv()
-        total += term_r[k].astype(F32)
-    ig_ref[...] = total.astype(BF16)
+    sum_terms()
 
     for op, ref in ((0, g_ref), (1, in_ref)):
         blocks_drain(op, ref)
@@ -656,12 +682,10 @@
     @pl.when(has_left)
     def _():
         to_left.wait_send()
-        corner_left.wait_send()
 
     @pl.when(has_right)
     def _():
         to_right.wait_send()
-        corner_right.wait_send()
 
     act_gather.drain()
     delta_gather.drain()
@@ -669,10 +693,9 @@
         @pl.loop(0, 9)
         def _(n):
             piece_gather(which, n).drain()
-            write_piece(which, n).wait()
-
-
-def join_kernel(dims, two_ref, one_ref, out_two, out_one):
+
+
+def join_kernel(dims, parts, out_two, out_one):
     nch, nsx, nsy, rows, lx, ly, nz = dims
     lane = ly * nz
     nk = nsx * nsy
@@ -685,17 +708,18 @@
     shape = (rest, lane)
     down = lax.broadcasted_iota(jnp.int32, shape, 0)
     picks = [(lanes(shape) == down + i * rest).astype(BF16) for i in range(2)]
-    for ref, out, mirror in ((two_ref, out_two, False), (one_ref, out_one, True)):
+    n = pl.program_id(0)
+    for which, out in ((0, out_two), (1, out_one)):
         for c in range(3):
-            to = 2 - c if mirror else c
+            to = 2 - c if which else c
             main, tail = [], []
             for k in range(nch):
                 for q in range(nk // 2):
                     slot = (2 * (q // 2) + k % 2) * nsy + q % 2
                     row = c * piece + (k // 2) * sub
-                    main.append(ref[slot, row : row + sub])
+                    main.append(parts[which, n, slot, pl.ds(row, sub)])
                     row = group + (row if row < group // 2 else row - group // 2)
-                    tail.append(ref[slot, row : row + sub])
+                    tail.append(parts[which, n, slot, pl.ds(row, sub)])
             half = len(main) // 2
             for i in range(2):
                 span = slice(i * half * sub, (i + 1) * half * sub)
@@ -731,25 +755,24 @@
         functools.partial(fused_kernel, dims, factor),
         out_shape=(
             jax.ShapeDtypeStruct(tile, BF16),
-            jax.ShapeDtypeStruct((2, 9, nk, size, lane), BF16),
+            pltpu.VMEM((2, 9, nk, size, lane), BF16),
         ),
         in_specs=[IN_VMEM] * 3 + [ANY] * 2,
-        out_specs=(IN_VMEM, ANY),
+        out_specs=(IN_VMEM, IN_VMEM),
         scratch_shapes=[
             vm(planes, nsy, rows, lane),
             vm(planes, nsy, rows, lane),
             vm(2, 2, nk, lx, piece // 2, lane),
             vm(nch, lx, rows, lane),
-            vm(2, nch, rows, lane),
-            vm(nch, lx // 2, rows, lane),
-            vm(nch, lx // 2, rows, lane),
-            vm(2, nch, rows, lane),
-            vm(3, lx + 2, channels, lane),
+            vm(2, rows, lane),
+            vm(2, rows, lane),
+            vm(lx // 2 + 1, rows, lane),
+            vm(lx // 2 + 1, rows, lane),
             vm(27, rows, channels),
-            vm(planes + 2, nsy, 9 * piece, lane),
-            pltpu.VMEM((9 * piece, 2 * lane), F32),
-            vm(2, 9, nk, size, lane),
-            pltpu.VMEM((3 * rows, npos), F32),
+            vm(3, planes + 2, nsy, 3 * piece, lane),
+            pltpu.VMEM((3 * piece, 2 * lane), F32),
+            pltpu.VMEM((3, lx + 2, 3 * rows, lane), F32),
+            pltpu.VMEM((lx + 2, rows, lane), F32),
             vm(lx, rows, lane),
             vm(lx + 2, ly + 2, nz, rows),
             pltpu.VMEM((3, npos, channels), F32),
@@ -758,27 +781,23 @@
             vm(nch, lx, rows, lane),
             dma(20, 8), dma(20, 8), dma(2, nk // 2), dma(2, nk), dma(2),
             dma(2, nch - 1), dma(2, 2), dma(nch - 1), dma(nch),
-            dma(5), dma(5), dma(nch - 1), dma(nch), dma(2), dma(2, 9),
+            dma(3), dma(3), dma(nch - 1), dma(nch), dma(2),
         ],
         compiler_params=pltpu.CompilerParams(
-            collective_id=0, has_side_effects=True, vmem_limit_bytes=62 * 1024 * 1024
+            collective_id=0, has_side_effects=True, vmem_limit_bytes=42 * 1024 * 1024
         ),
     )(tiles(out_grad), tiles(inputs), tiles(active), weight_one, weight_two)
-    block = (None, None, nk, size, lane)
     two, one = pl.pallas_call(
         functools.partial(join_kernel, dims),
         grid=(9,),
         out_shape=(jax.ShapeDtypeStruct((27, rows, channels), F32),) * 2,
-        in_specs=[
-            pl.BlockSpec(block, lambda n: (0, n, 0, 0, 0)),
-            pl.BlockSpec(block, lambda n: (1, n, 0, 0, 0)),
-        ],
+        in_specs=[IN_VMEM],
         out_specs=(
             pl.BlockSpec((3, rows, channels), lambda n: (n, 0, 0)),
             pl.BlockSpec((3, rows, channels), lambda n: (8 - n, 0, 0)),
         ),
-        compiler_params=pltpu.CompilerParams(vmem_limit_bytes=40 * 1024 * 1024),
-    )(pieces, pieces)
+        compiler_params=pltpu.CompilerParams(vmem_limit_bytes=20 * 1024 * 1024),
+    )(pieces)
     grad = grad.transpose(1, 0, 2).reshape(rows, lx, ly, nz)
     return grad, one, two
 

time: 160 us -> 144 us (0.900)
  Pallas kernels: 152 us -> 137 us
    pallas_call x1, Pallas kernels: 133 us -> 123 us  [fused_shards(): pl.pallas_call(functools.partial(fused_kernel, dims, factor), out_shape=(...]
    pallas_call x1, Pallas kernels: 19.6 us -> 13.6 us  [fused_shards(): pl.pallas_call(functools.partial(join_kernel, dims), grid=(9,), out_shape...]
where the time goes in v1:
time: 144 us
  Pallas kernels  137 us (95%)
  local copies, waits for them, and re-layouts  5.2 us (4%)
    pallas_call x1, Pallas kernels, fused_shards(): pl.pallas_call(functools.partial(fused_kernel, dims, factor), out_shape=(...  123 us
    pallas_call x1, Pallas kernels, fused_shards(): pl.pallas_call(functools.partial(join_kernel, dims), grid=(9,), out_shape...  13.6 us
    reshape x3, local copies, waits for them, and re-layouts, tiles(): return array.reshape(rows, lx, ly * nz).transpose(1, 0, 2)  4.34 us

profile of v1, /device:TPU:25, one launch (start us, length us, event | category | flops | bytes accessed | tf_op | source)
XLA Modules:
  0.0 143.8 jit_solution(11824117263297783757)
XLA Ops:
  0.6 1.0 broadcast_maximum_fusion
  1.6 0.8 copy.14
  2.4 1.8 %copy.12 = bf16[192,4,128]{2,0,1:T(8,128)(2,1)} copy(bf16[192,4,128]{0,2,1:T(8,128)(2,1)} %bitcast.12) | data formatting | bytes 393216 | tf_op jit(solution)/shard_map/reshape | solution.py:735
  4.2 1.8 %copy.13 = bf16[192,4,128]{2,0,1:T(8,128)(2,1)} copy(bf16[192,4,128]{0,2,1:T(8,128)(2,1)} %bitcast.13) | data formatting | bytes 393216 | tf_op jit(solution)/shard_map/reshape | solution.py:735
  5.9 123.5 %shard_map.76 = (bf16[4,192,128]{2,1,0:T(8,128)(2,1)}, bf16[2,9,8,432,128]{4,3,2,1,0:T(8,128)(2,1)S(1)}) custom-call(bf16[4,192,128]{2,1,0:T(8,128)(2,1)} %bitcast.10, bf16[4,192,128]{2,1,0:T(8,128)(2,1)} %bitcast.11, bf16[4,192,128]{2,1,0:T(8,128)(2,1)} %bitcast.9, bf16[27,192,768]{2,1,0:T(8,128)(2,1)} %w1_hbm.1, bf16[27,192,768]{2,1,0:T(8,128)(2,1)} %w2_hbm.1), custom_call_target="tpu_custom_call" | custom-call | tf_op jit(solution)/shard_map/pallas_call | solution.py:754
  129.4 0.0 copy-start
  129.4 13.6 %shard_map.77 = (f32[27,192,768]{2,1,0:T(8,128)}, f32[27,192,768]{2,1,0:T(8,128)}) custom-call(bf16[2,9,8,432,128]{4,3,2,1,0:T(8,128)(2,1)S(1)} %get-tuple-element.8.parts), custom_call_target="tpu_custom_call" | custom-call | tf_op jit(solution)/shard_map/pallas_call | solution.py:790
  143.0 0.0 copy-done
  143.0 0.8 copy.15
Async XLA Ops:
  129.4 13.6 %copy-start = (bf16[4,192,128]{2,1,0:T(8,128)(2,1)S(1)}, bf16[4,192,128]{2,1,0:T(8,128)(2,1)}, u32[]{:S(2)}) copy-start(bf16[4,192,128]{2,1,0:T(8,128)(2,1)} %get-tuple-element.7) | copy-start | bytes 589828

commit v2 on v1

--- a/solution.py
+++ b/solution.py
@@ -237,13 +237,14 @@
 
 def fused_kernel(
     dims, factor,
-    g_ref, in_ref, act_ref, w1_hbm, w2_hbm,
+    own_ref, w1_hbm, w2_hbm,
     ig_ref, parts,
     acts, deltas, cols, full, edge_s, edge_r, pack_s, pack_r, weight, shifted,
     facc, cacc, near, dl, dpos, zacc, igt, term_s, term_r,
     ag_s, ag_r, c1_s, c1_r, c1_l, c2_s, c2_r, g_s, g_r, h_s, h_r, t_s, t_r, w_sem,
 ):
     nch, nsx, nsy, rows, lx, ly, nz = dims
+    g_ref, in_ref, act_ref = (own_ref.at[:, pl.ds(i * rows, rows)] for i in range(3))
     lane = ly * nz
     nk = nsx * nsy
     piece = rows * nch // nk
@@ -335,15 +336,14 @@
             for step in range(1, nch):
                 spread_copy(op, step).start()
 
-    def spread_wait(op):
-        for t in range(2):
-            @pl.when(core + 2 * t != z)
-            def _():
-                block = cols.at[op, t]
-                pltpu.make_async_remote_copy(
-                    src_ref=block, dst_ref=block, send_sem=c2_s.at[op, 0], recv_sem=c2_r.at[op, t],
-                    device_id=here, device_id_type=MESH,
-                ).wait_recv()
+    def spread_wait(op, t):
+        @pl.when(core + 2 * t != z)
+        def _():
+            block = cols.at[op, t]
+            pltpu.make_async_remote_copy(
+                src_ref=block, dst_ref=block, send_sem=c2_s.at[op, 0], recv_sem=c2_r.at[op, t],
+                device_id=here, device_id_type=MESH,
+            ).wait_recv()
 
     def spread_drain(op):
         @pl.when(parity == core)
@@ -351,11 +351,44 @@
             for step in range(1, nch):
                 spread_copy(op, step).wait_send()
 
-    def full_copy(step):
-        return pltpu.make_async_remote_copy(
-            src_ref=g_ref, dst_ref=full.at[z], send_sem=g_s.at[step - 1], recv_sem=g_r.at[z],
-            device_id=(lax.rem(z + step, nch), s, y), device_id_type=MESH,
-        )
+    def full_pass(hop, to):
+        k = z - hop if to else z + hop
+        valid = jnp.logical_and(k >= 0, z < nch - 1) if to else jnp.logical_and(k < nch, z > 0)
+        k = jnp.clip(k, 0, nch - 1)
+        copy = pltpu.make_async_remote_copy(
+            src_ref=g_ref if hop == 0 else full.at[k], dst_ref=full.at[k],
+            send_sem=g_s.at[hop, to], recv_sem=g_r.at[k],
+            device_id=(jnp.clip(z + 2 * to - 1, 0, nch - 1), s, y), device_id_type=MESH,
+        )
+        return valid, copy
+
+    def start_full(hop):
+        for to in range(2):
+            valid, copy = full_pass(hop, to)
+
+            @pl.when(valid)
+            def _():
+                copy.start()
+
+    def drain_full():
+        for hop in range(nch - 1):
+            for to in range(2):
+                valid, copy = full_pass(hop, to)
+
+                @pl.when(valid)
+                def _():
+                    copy.wait_send()
+
+    def wait_full(hop):
+        for k, valid in ((z - hop, z >= hop), (z + hop, z + hop < nch)):
+            k = jnp.clip(k, 0, nch - 1)
+
+            @pl.when(valid)
+            def _():
+                pltpu.make_async_remote_copy(
+                    src_ref=full.at[k], dst_ref=full.at[k], send_sem=g_s.at[0, 0],
+                    recv_sem=g_r.at[k], device_id=here, device_id_type=MESH,
+                ).wait_recv()
 
     def whole(ref):
         slot = lambda k: ref.at[pl.ds(lx * k[0], lx), k[1]]
@@ -372,12 +405,12 @@
         half = lambda k, i: parts.at[
             which, n, k[0] * nsy + k[1], pl.ds(0, cut) if i == 0 else pl.ds(cut, size - cut)
         ]
-        return Gather(2 + 9 * which + n, slot((s, y)), slot, half, ag_s, ag_r, here)
+        return Gather(2 + 6 * which + n, slot((s, y)), slot, half, ag_s, ag_r, here)
 
     def clear():
-        for b in range(3):
+        for t in range(2):
             for p in (0, nsx * lx + 1):
-                shifted[b, p] = jnp.zeros(shifted.shape[2:], BF16)
+                shifted[t, p] = jnp.zeros(shifted.shape[2:], BF16)
         facc[...] = jnp.zeros(facc.shape, F32)
         for b in range(3):
             for x in range(lx + 2):
@@ -386,75 +419,68 @@
         acts[pl.ds(lx * s, lx), y] = act_ref[...]
         full[z] = g_ref[...]
 
-    def start_full(beside):
-        for step in range(1, nch):
-            next_to = {1: z < nch - 1, nch - 1: z > 0}.get(step, z < 0)
-
-            @pl.when(next_to if beside else jnp.logical_not(next_to))
-            def _():
-                full_copy(step).start()
-
-    def shift_columns(op, b):
+    def shift_columns(op, t):
         @pl.loop(0, nsx * lx)
         def _(p):
             owner, inner = p // lx, lax.rem(p, lx)
-            tiles = [
-                jnp.concatenate([cols[op, t, owner * nsy + j, inner] for t in range(2)], axis=0)
-                for j in range(nsy)
-            ]
+            tiles = [cols[op, t, owner * nsy + j, inner] for j in range(nsy)]
             plane = jnp.concatenate(tiles, axis=1).astype(F32)
-            where = lanes((piece, wide))
+            where = lanes((sub, wide))
             row, depth = where // nz, lax.rem(where, nz)
-            for c in range(3):
-                move = (nz * (b - 1) + c - 1) % wide
-                value = pltpu.roll(plane, move, 1) if move else plane
-                keep = where >= 0
-                if b == 0:
-                    keep = jnp.logical_and(keep, row < nsy * ly - 1)
-                if b == 2:
-                    keep = jnp.logical_and(keep, row > 0)
-                if c == 0:
-                    keep = jnp.logical_and(keep, depth < nz - 1)
-                if c == 2:
-                    keep = jnp.logical_and(keep, depth > 0)
-                value = jnp.where(keep, value, 0.0).astype(BF16)
-                for j in range(nsy):
-                    shifted[b, p + 1, j, pl.ds(c * piece, piece)] = value[:, j * lane : (j + 1) * lane]
-
-    def filter_pieces(which, left, b):
+            for b in range(3):
+                for c in range(3):
+                    move = (nz * (b - 1) + c - 1) % wide
+                    value = pltpu.roll(plane, move, 1) if move else plane
+                    keep = where >= 0
+                    if b == 0:
+                        keep = jnp.logical_and(keep, row < nsy * ly - 1)
+                    if b == 2:
+                        keep = jnp.logical_and(keep, row > 0)
+                    if c == 0:
+                        keep = jnp.logical_and(keep, depth < nz - 1)
+                    if c == 2:
+                        keep = jnp.logical_and(keep, depth > 0)
+                    value = jnp.where(keep, value, 0.0).astype(BF16)
+                    for j in range(nsy):
+                        shifted[t, p + 1, j, pl.ds((3 * b + c) * sub, sub)] = value[
+                            :, j * lane : (j + 1) * lane
+                        ]
+
+    def filter_pieces(which, left, t):
         @pl.loop(0, 3)
         def _(a):
             facc[:, :rows] = jnp.zeros((facc.shape[0], rows), F32)
 
             @pl.loop(0, nsx)
             def _(o):
-                cells = shifted[b, pl.ds(2 - a + lx * o, lx)]
+                cells = shifted[t, pl.ds(2 - a + lx * o, lx)]
                 other = left[pl.ds(lx * o, lx)]
                 cells = jnp.concatenate([cells[i, j] for i in range(lx) for j in range(nsy)], axis=1)
                 other = jnp.concatenate([other[i, j] for i in range(lx) for j in range(nsy)], axis=1)
                 facc[:, :rows] += dot_lanes(cells, other)
 
-            group = 3 * piece
-            n = 3 * a + b
+            group = 9 * sub
+            n = 3 * t + a
             parts[which, n, mine, pl.ds(0, group)] = (facc[:, :lane] * factor).astype(BF16)
-            low = facc[: group // 2, lane : 2 * lane] * factor
-            high = facc[group // 2 :, lane : 2 * lane] * factor
-            both = jnp.where(lanes(low.shape) < rows - lane, low, swap_halves(high))
-            parts[which, n, mine, pl.ds(group, group // 2)] = both.astype(BF16)
+            for low, high, size_of, to in ((0, 4 * sub, 4 * sub, 0), (8 * sub, 17 * sub // 2, sub // 2, 4 * sub)):
+                first = facc[pl.ds(low, size_of), lane : 2 * lane] * factor
+                second = facc[pl.ds(high, size_of), lane : 2 * lane] * factor
+                both = jnp.where(lanes(first.shape) < rows - lane, first, swap_halves(second))
+                parts[which, n, mine, pl.ds(group + to, size_of)] = both.astype(BF16)
             piece_gather(which, n).start()
 
-    def relay_pieces(which, b):
+    def relay_pieces(which, t):
         @pl.loop(0, 3)
         def _(a):
-            piece_gather(which, 3 * a + b).relay()
-
-    def far_pieces(which, b):
+            piece_gather(which, 3 * t + a).relay()
+
+    def far_pieces(which, t):
         @pl.loop(0, 3)
         def _(a):
-            piece_gather(which, 3 * a + b).relay_far()
-
-    def finish_pieces(which, first, last):
-        @pl.loop(first, last)
+            piece_gather(which, 3 * t + a).relay_far()
+
+    def finish_pieces(which):
+        @pl.loop(0, 6)
         def _(n):
             piece_gather(which, n).finish()
 
@@ -480,14 +506,6 @@
             src_ref=term_s.at[to], dst_ref=term_r.at[z], send_sem=t_s.at[step - 1],
             recv_sem=t_r.at[z], device_id=(to, s, y), device_id_type=MESH,
         )
-
-    def wait_full():
-        for step in range(1, nch):
-            k = lax.rem(z + step, nch)
-            pltpu.make_async_remote_copy(
-                src_ref=full.at[k], dst_ref=full.at[k], send_sem=g_s.at[0], recv_sem=g_r.at[k],
-                device_id=here, device_id_type=MESH,
-            ).wait_recv()
 
     def act_grad():
         load_two.wait()
@@ -577,10 +595,8 @@
                 dpos[x, 1 + j] = own[j * nz : (j + 1) * nz]
             dpos[x, ly + 1] = jnp.where(y == 0, beside, 0.0).astype(BF16)
 
-    def input_terms():
-        load_one.wait()
-
-        @pl.loop(0, 9)
+    def input_terms(first, last):
+        @pl.loop(first, last)
         def _(ab):
             a, b = ab // 3, lax.rem(ab, 3)
             left = dpos[pl.ds(2 - a, lx), pl.ds(2 - b, ly)].reshape(npos, rows)
@@ -618,116 +634,145 @@
             total += term_r[k].astype(F32)
         ig_ref[...] = total.astype(BF16)
 
+    def drain_columns():
+        for op, ref in ((0, g_ref), (1, in_ref)):
+            blocks_drain(op, ref)
+            spread_drain(op)
+        drain_full()
+
+    def drain_halo():
+        for step in range(1, nch):
+            term_copy(step).wait_send()
+        to_y.wait_send()
+
+        @pl.when(has_left)
+        def _():
+            to_left.wait_send()
+
+        @pl.when(has_right)
+        def _():
+            to_right.wait_send()
+
+        act_gather.drain()
+        delta_gather.drain()
+
+    def drain_pieces(which):
+        @pl.loop(0, 6)
+        def _(n):
+            piece_gather(which, n).drain()
+
     blocks_start(0, g_ref)
     act_gather.start()
-    start_full(True)
-    blocks_start(1, in_ref)
+    start_full(0)
     blocks_wait(0, g_ref)
     spread_start(0)
     clear()
     act_gather.relay()
+
+    @pl.when(parity == core)
+    def _():
+        shift_columns(0, turn)
+
     act_gather.relay_far()
     act_gather.finish()
-    spread_wait(0)
-    start_full(False)
-    shift_columns(0, 1)
-    filter_pieces(0, acts, 1)
-    shift_columns(0, 2)
-    filter_pieces(0, acts, 2)
-    relay_pieces(0, 1)
-    shift_columns(0, 0)
+
+    @pl.when(parity != core)
+    def _():
+        spread_wait(0, turn)
+        shift_columns(0, turn)
+
+    filter_pieces(0, acts, turn)
+    spread_wait(0, 1 - turn)
+    wait_full(1)
+    start_full(1)
+    blocks_start(1, in_ref)
+    shift_columns(0, 1 - turn)
+    relay_pieces(0, turn)
+    wait_full(2)
+    start_full(2)
+    filter_pieces(0, acts, 1 - turn)
     blocks_wait(1, in_ref)
-    wait_full()
+    wait_full(3)
     spread_start(1)
     act_grad()
     fold_halo()
-    relay_pieces(0, 2)
     fold_edges()
     make_delta()
-    filter_pieces(0, acts, 0)
+    relay_pieces(0, 1 - turn)
+    far_pieces(0, turn)
     delta_gather.relay()
-    spread_wait(1)
-    shift_columns(1, 1)
+    spread_wait(1, turn)
+    shift_columns(1, turn)
     delta_gather.relay_far()
-    relay_pieces(0, 0)
-    shift_columns(1, 2)
+    spread_wait(1, 1 - turn)
+    shift_columns(1, 1 - turn)
     delta_gather.finish()
-    filter_pieces(1, deltas, 1)
-    filter_pieces(1, deltas, 2)
-    shift_columns(1, 0)
-    for b in (1, 2, 0):
-        far_pieces(0, b)
-    relay_pieces(1, 1)
+    filter_pieces(1, deltas, turn)
+    far_pieces(0, 1 - turn)
     place_delta()
-    input_terms()
+    load_one.wait()
+    input_terms(0, 9)
     pack_terms()
     send_terms()
-    finish_pieces(0, 0, 9)
-    filter_pieces(1, deltas, 0)
-    relay_pieces(1, 2)
-    relay_pieces(1, 0)
-    for b in range(3):
-        far_pieces(1, (b + 1) % 3)
-    finish_pieces(1, 0, 9)
+    relay_pieces(1, turn)
+    filter_pieces(1, deltas, 1 - turn)
+    finish_pieces(0)
+    drain_columns()
+    drain_pieces(0)
+    relay_pieces(1, 1 - turn)
+    far_pieces(1, turn)
+    far_pieces(1, 1 - turn)
     sum_terms()
-
-    for op, ref in ((0, g_ref), (1, in_ref)):
-        blocks_drain(op, ref)
-        spread_drain(op)
-    for step in range(1, nch):
-        full_copy(step).wait_send()
-        term_copy(step).wait_send()
-    to_y.wait_send()
-
-    @pl.when(has_left)
-    def _():
-        to_left.wait_send()
-
-    @pl.when(has_right)
-    def _():
-        to_right.wait_send()
-
-    act_gather.drain()
-    delta_gather.drain()
-    for which in range(2):
-        @pl.loop(0, 9)
-        def _(n):
-            piece_gather(which, n).drain()
+    drain_halo()
+    finish_pieces(1)
+    drain_pieces(1)
 
 
 def join_kernel(dims, parts, out_two, out_one):
     nch, nsx, nsy, rows, lx, ly, nz = dims
     lane = ly * nz
     nk = nsx * nsy
-    piece = rows * nch // nk
-    sub = piece // 2
-    group = 3 * piece
+    sub = rows * nch // nk // 2
+    group = 9 * sub
     rest = rows - lane
+    a = pl.program_id(0) // 3
     shape = (lane, lane)
     same = (lanes(shape) == lax.broadcasted_iota(jnp.int32, shape, 0)).astype(BF16)
     shape = (rest, lane)
-    down = lax.broadcasted_iota(jnp.int32, shape, 0)
-    picks = [(lanes(shape) == down + i * rest).astype(BF16) for i in range(2)]
-    n = pl.program_id(0)
-    for which, out in ((0, out_two), (1, out_one)):
-        for c in range(3):
-            to = 2 - c if which else c
-            main, tail = [], []
-            for k in range(nch):
-                for q in range(nk // 2):
-                    slot = (2 * (q // 2) + k % 2) * nsy + q % 2
-                    row = c * piece + (k // 2) * sub
-                    main.append(parts[which, n, slot, pl.ds(row, sub)])
-                    row = group + (row if row < group // 2 else row - group // 2)
-                    tail.append(parts[which, n, slot, pl.ds(row, sub)])
-            half = len(main) // 2
-            for i in range(2):
-                span = slice(i * half * sub, (i + 1) * half * sub)
-                part = jnp.concatenate(main[i * half : (i + 1) * half], axis=0)
-                out[to, :lane, span] = dot_lanes(same, part)
-                part = jnp.concatenate(tail[i * half : (i + 1) * half], axis=0)
-                upper = c * piece + i * sub >= group // 2
-                out[to, lane:, span] = dot_lanes(picks[1 if upper else 0], part)
+    down, across = lax.broadcasted_iota(jnp.int32, shape, 0), lanes(shape)
+    picks = [(across == down).astype(BF16), (across == down + rest).astype(BF16)]
+    shape = (sub, lane)
+    own_half = lax.broadcasted_iota(jnp.int32, shape, 0) // (sub // 2) == lanes(shape) // rest
+
+    def gathered(which, load):
+        found = []
+        for k in range(nch):
+            for q in range(nk // 2):
+                slot = (2 * (q // 2) + k % 2) * nsy + q % 2
+                found.append(load((which, 3 * (k // 2) + a, slot)))
+        return jnp.concatenate(found, axis=0)
+
+    def join(b, c, which, out):
+        block = 3 * b + c
+        out[:lane] = dot_lanes(same, gathered(which, lambda at: parts[(*at, pl.ds(block * sub, sub))]))
+        start = group + block % 4 * sub
+        if block < 8:
+            tail = gathered(which, lambda at: parts[(*at, pl.ds(start, sub))])
+            out[lane:] = dot_lanes(picks[block // 4], tail)
+        else:
+            def load(at):
+                half = parts[(*at, pl.ds(group + 4 * sub, sub // 2))].astype(F32)
+                both = jnp.concatenate([half, half], axis=0)
+                return jnp.where(own_half, both, 0.0).astype(BF16)
+
+            out[lane:] = dot_lanes(picks[0] + picks[1], gathered(which, load))
+
+    for b in range(3):
+        @pl.when(lax.rem(pl.program_id(0), 3) == b)
+        def _():
+            for c in range(3):
+                join(b, c, 0, out_two.at[c])
+                join(b, c, 1, out_one.at[2 - c])
 
 
 def tiles(array):
@@ -745,19 +790,20 @@
     piece = channels // nk
     npos = lx * lane
     factor = 1.0 / math.sqrt(npos * nk)
-    size = 3 * piece * rows // lane
+    size = 9 * piece // 2 * rows // lane
     planes = nsx * lx
     tile = (lx, rows, lane)
     vm = lambda *shape: pltpu.VMEM(shape, BF16)
     dma = lambda *shape: pltpu.SemaphoreType.DMA(shape)
     active = jnp.maximum(pre_act, jnp.zeros((), pre_act.dtype))
+    own = tiles(jnp.concatenate([out_grad, inputs, active], axis=0))
     grad, pieces = pl.pallas_call(
         functools.partial(fused_kernel, dims, factor),
         out_shape=(
             jax.ShapeDtypeStruct(tile, BF16),
-            pltpu.VMEM((2, 9, nk, size, lane), BF16),
+            pltpu.VMEM((2, 6, nk, size, lane), BF16),
         ),
-        in_specs=[IN_VMEM] * 3 + [ANY] * 2,
+        in_specs=[IN_VMEM] + [ANY] * 2,
         out_specs=(IN_VMEM, IN_VMEM),
         scratch_shapes=[
             vm(planes, nsy, rows, lane),
@@ -769,8 +815,8 @@
             vm(lx // 2 + 1, rows, lane),
             vm(lx // 2 + 1, rows, lane),
             vm(27, rows, channels),
-            vm(3, planes + 2, nsy, 3 * piece, lane),
-            pltpu.VMEM((3 * piece, 2 * lane), F32),
+            vm(2, planes + 2, nsy, 9 * piece // 2, lane),
+            pltpu.VMEM((9 * piece // 2, 2 * lane), F32),
             pltpu.VMEM((3, lx + 2, 3 * rows, lane), F32),
             pltpu.VMEM((lx + 2, rows, lane), F32),
             vm(lx, rows, lane),
@@ -779,14 +825,14 @@
             vm(npos, channels),
             vm(nch, lx, rows, lane),
             vm(nch, lx, rows, lane),
-            dma(20, 8), dma(20, 8), dma(2, nk // 2), dma(2, nk), dma(2),
-            dma(2, nch - 1), dma(2, 2), dma(nch - 1), dma(nch),
+            dma(14, 8), dma(14, 8), dma(2, nk // 2), dma(2, nk), dma(2),
+            dma(2, nch - 1), dma(2, 2), dma(nch - 1, 2), dma(nch),
             dma(3), dma(3), dma(nch - 1), dma(nch), dma(2),
         ],
         compiler_params=pltpu.CompilerParams(
             collective_id=0, has_side_effects=True, vmem_limit_bytes=42 * 1024 * 1024
         ),
-    )(tiles(out_grad), tiles(inputs), tiles(active), weight_one, weight_two)
+    )(own, weight_one, weight_two)
     two, one = pl.pallas_call(
         functools.partial(join_kernel, dims),
         grid=(9,),

time: 144 us -> 131 us (0.910); the launches traced: 144 us -> 129 us
  Pallas kernels: 137 us -> 124 us
  local copies, waits for them, and re-layouts: 5.2 us -> 1.91 us
    pallas_call x1, Pallas kernels: 123 us -> 111 us  [fused_shards(): pl.pallas_call(functools.partial(fused_kernel, dims, factor), out_shape=(...]
    reshape x3 -> x1, local copies, waits for them, and re-layouts: 4.34 us -> 1.06 us  [tiles(): return array.reshape(rows, lx, ly * nz).transpose(1, 0, 2)]
where the time goes in v2:
time: 131 us; the launch traced here: 129 us
  Pallas kernels  124 us (95%)
  other arithmetic  2.22 us (2%)
  local copies, waits for them, and re-layouts  1.91 us (1%)
    pallas_call x1, Pallas kernels, fused_shards(): pl.pallas_call(functools.partial(fused_kernel, dims, factor), out_shape=(...  111 us
    pallas_call x1, Pallas kernels, fused_shards(): pl.pallas_call(functools.partial(join_kernel, dims), grid=(9,), out_shape...  13.2 us

profile of v2, /device:TPU:25, one launch (start us, length us, event | category | flops | bytes accessed | tf_op | source)
XLA Modules:
  0.0 129.3 jit_solution(15353102453006487703)
XLA Ops:
  0.6 1.0 broadcast_maximum_fusion
  1.6 1.3 pad_maximum_fusion
  2.9 1.1 copy.10
  3.9 111.3 %shard_map.76 = (bf16[4,192,128]{2,1,0:T(8,128)(2,1)}, bf16[2,6,8,648,128]{4,3,2,1,0:T(8,128)(2,1)S(1)}) custom-call(bf16[4,576,128]{2,1,0:T(8,128)(2,1)} %bitcast.5, bf16[27,192,768]{2,1,0:T(8,128)(2,1)} %w1_hbm.1, bf16[27,192,768]{2,1,0:T(8,128)(2,1)} %w2_hbm.1), custom_call_target="tpu_custom_call" | custom-call | tf_op jit(solution)/shard_map/pallas_call | solution.py:800
  115.2 0.0 copy-start
  115.2 13.2 %shard_map.77 = (f32[27,192,768]{2,1,0:T(8,128)}, f32[27,192,768]{2,1,0:T(8,128)}) custom-call(bf16[2,6,8,648,128]{4,3,2,1,0:T(8,128)(2,1)S(1)} %get-tuple-element.8.parts), custom_call_target="tpu_custom_call" | custom-call | tf_op jit(solution)/shard_map/pallas_call | solution.py:836
  128.4 0.0 copy-done
  128.4 0.8 copy.11
Async XLA Ops:
  115.2 13.2 %copy-start = (bf16[4,192,128]{2,1,0:T(8,128)(2,1)S(1)}, bf16[4,192,128]{2,1,0:T(8,128)(2,1)}, u32[]{:S(2)}) copy-start(bf16[4,192,128]{2,1,0:T(8,128)(2,1)} %get-tuple-element.7) | copy-start | bytes 589828

commit v3 on v2

--- a/solution.py
+++ b/solution.py
@@ -160,7 +160,7 @@
 
 
 class Gather:
-    def __init__(self, index, own, slot, half, send, recv, here):
+    def __init__(self, index, own, slot, half, several, send, recv, here):
         z, s, y = here
         flip = lax.rem(s + 2, 4)
         other = s + 1 - 2 * lax.rem(s, 2)
@@ -169,14 +169,14 @@
         self.mine, self.from_x, self.from_y, self.from_d = (s, y), (flip, y), (s, 1 - y), (flip, 1 - y)
         self.pair = [(other, y), (other_flip, y), (other, 1 - y), (other_flip, 1 - y)]
         self.index, self.own, self.slot, self.half = index, own, slot, half
-        self.send, self.recv = send, recv
+        self.send, self.recv, self.several = send, recv, several
 
     def copy(self, step, src, dst, to):
         return pltpu.make_async_remote_copy(
             src_ref=src,
             dst_ref=dst,
-            send_sem=self.send.at[self.index, step],
-            recv_sem=self.recv.at[self.index, step],
+            send_sem=self.send.at[self.index],
+            recv_sem=self.recv.at[self.index, (0, 1, 3, 2, 2, 3, 3, 3)[step]],
             device_id=self.near[to],
             device_id_type=MESH,
         )
@@ -203,12 +203,8 @@
         where = {
             0: lambda: self.slot(self.from_x),
             1: lambda: self.slot(self.from_y),
-            2: lambda: self.slot(self.pair[0]),
-            3: lambda: self.half(self.from_d, 0),
-            4: lambda: self.half(self.from_d, 1),
-            5: lambda: self.slot(self.pair[1]),
-            6: lambda: self.slot(self.pair[2]),
-            7: lambda: self.slot(self.pair[3]),
+            2: lambda: self.several(4),
+            3: lambda: self.slot(self.from_d),
         }[step]()
         self.copy(step, where, where, 0).wait_recv()
 
@@ -223,16 +219,14 @@
 
     def relay_far(self):
         self.arrive(3)
-        self.arrive(4)
         self.begin((7,))
 
     def finish(self):
-        for step in (2, 5, 6, 7):
-            self.arrive(step)
+        self.arrive(2)
 
     def drain(self):
-        for entry in self.sends():
-            self.copy(*entry).wait_send()
+        sent = self.several(7)
+        self.copy(0, sent, sent, 0).wait_send()
 
 
 def fused_kernel(
@@ -393,7 +387,8 @@
     def whole(ref):
         slot = lambda k: ref.at[pl.ds(lx * k[0], lx), k[1]]
         half = lambda k, i: ref.at[pl.ds(lx * k[0] + i * (lx // 2), lx // 2), k[1]]
-        return slot, half
+        several = lambda n: ref.at[pl.ds(0, lx * n // nsy)]
+        return slot, half, several
 
     act_gather = Gather(0, act_ref, *whole(acts), ag_s, ag_r, here)
     delta_gather = Gather(1, dl, *whole(deltas), ag_s, ag_r, here)
@@ -405,7 +400,8 @@
         half = lambda k, i: parts.at[
             which, n, k[0] * nsy + k[1], pl.ds(0, cut) if i == 0 else pl.ds(cut, size - cut)
         ]
-        return Gather(2 + 6 * which + n, slot((s, y)), slot, half, ag_s, ag_r, here)
+        several = lambda count: parts.at[which, n, pl.ds(0, count)]
+        return Gather(2 + 6 * which + n, slot((s, y)), slot, half, several, ag_s, ag_r, here)
 
     def clear():
         for t in range(2):
@@ -446,8 +442,8 @@
                             :, j * lane : (j + 1) * lane
                         ]
 
-    def filter_pieces(which, left, t):
-        @pl.loop(0, 3)
+    def filter_pieces(which, left, t, first=0, last=3):
+        @pl.loop(first, last)
         def _(a):
             facc[:, :rows] = jnp.zeros((facc.shape[0], rows), F32)
 
@@ -668,6 +664,7 @@
     spread_start(0)
     clear()
     act_gather.relay()
+    blocks_start(1, in_ref)
 
     @pl.when(parity == core)
     def _():
@@ -685,12 +682,12 @@
     spread_wait(0, 1 - turn)
     wait_full(1)
     start_full(1)
-    blocks_start(1, in_ref)
     shift_columns(0, 1 - turn)
-    relay_pieces(0, turn)
+    filter_pieces(0, acts, 1 - turn, 0, 1)
     wait_full(2)
     start_full(2)
-    filter_pieces(0, acts, 1 - turn)
+    filter_pieces(0, acts, 1 - turn, 1, 3)
+    relay_pieces(0, turn)
     blocks_wait(1, in_ref)
     wait_full(3)
     spread_start(1)
@@ -825,7 +822,7 @@
             vm(npos, channels),
             vm(nch, lx, rows, lane),
             vm(nch, lx, rows, lane),
-            dma(14, 8), dma(14, 8), dma(2, nk // 2), dma(2, nk), dma(2),
+            dma(14), dma(14, 4), dma(2, nk // 2), dma(2, nk), dma(2),
             dma(2, nch - 1), dma(2, 2), dma(nch - 1, 2), dma(nch),
             dma(3), dma(3), dma(nch - 1), dma(nch), dma(2),
         ],

time: 131 us -> 129 us (0.985)
  the two profiles are of different devices: /device:TPU:25 before, /device:TPU:17 now
where the time goes in v3:
time: 129 us
  Pallas kernels  124 us (96%)
  other arithmetic  2.22 us (2%)
  local copies, waits for them, and re-layouts  1.91 us (1%)
    pallas_call x1, Pallas kernels, fused_shards(): pl.pallas_call(functools.partial(fused_kernel, dims, factor), out_shape=(...  111 us
    pallas_call x1, Pallas kernels, fused_shards(): pl.pallas_call(functools.partial(join_kernel, dims), grid=(9,), out_shape...  13.2 us

profile of v3, /device:TPU:17, one launch (start us, length us, event | category | flops | bytes accessed | tf_op | source)
XLA Modules:
  0.0 129.0 jit_solution(5928795367422238676)
XLA Ops:
  0.6 1.0 broadcast_maximum_fusion
  1.6 1.3 pad_maximum_fusion
  2.9 1.1 copy.10
  3.9 111.0 %shard_map.76 = (bf16[4,192,128]{2,1,0:T(8,128)(2,1)}, bf16[2,6,8,648,128]{4,3,2,1,0:T(8,128)(2,1)S(1)}) custom-call(bf16[4,576,128]{2,1,0:T(8,128)(2,1)} %bitcast.5, bf16[27,192,768]{2,1,0:T(8,128)(2,1)} %w1_hbm.1, bf16[27,192,768]{2,1,0:T(8,128)(2,1)} %w2_hbm.1), custom_call_target="tpu_custom_call" | custom-call | tf_op jit(solution)/shard_map/pallas_call | solution.py:797
  114.9 0.0 copy-start
  114.9 13.2 %shard_map.77 = (f32[27,192,768]{2,1,0:T(8,128)}, f32[27,192,768]{2,1,0:T(8,128)}) custom-call(bf16[2,6,8,648,128]{4,3,2,1,0:T(8,128)(2,1)S(1)} %get-tuple-element.8.parts), custom_call_target="tpu_custom_call" | custom-call | tf_op jit(solution)/shard_map/pallas_call | solution.py:833
  128.1 0.0 copy-done
  128.1 0.8 copy.11
Async XLA Ops:
  114.9 13.2 %copy-start = (bf16[4,192,128]{2,1,0:T(8,128)(2,1)S(1)}, bf16[4,192,128]{2,1,0:T(8,128)(2,1)}, u32[]{:S(2)}) copy-start(bf16[4,192,128]{2,1,0:T(8,128)(2,1)} %get-tuple-element.7) | copy-start | bytes 589828
